TPU v7x, 256 devices: a whole 4x4x8 slice. The times are simulated.
256 devices in a mesh: dop: 8 (over z_lo, core), tm: 32 (over y, x, z_hi).
Axes of the slice: x: 4, y: 4, z: 8 (z_hi: 2, z_lo: 4; z = z_hi * 4 + z_lo), core: 2. Of those that a mesh axis runs over, the one named last changes fastest.
Arguments:
- surveillance: bfloat16 [2, 32, 8192], P(None, 'tm', 'dop'), may hold values from -6 to 6
- reference_signal: bfloat16 [2, 32, 8192], P(None, 'tm', 'dop'), may hold values from -6 to 6
Outputs:
- ambiguity: float32 [2048, 2, 512], P('tm', None, 'dop')
All inputs are finite; a program needn't handle non-finite values.
Results may differ from a plain program's by a relative error of at most 0.0029.
Values may be sent and summed in bfloat16 or wider, within the bound.
A program may use at most 128 MiB of HBM per device.

v0:
```python
import math

import jax
import jax.numpy as jnp
from jax import lax
from jax.sharding import PartitionSpec as P

F = 512
LAGS = 2048
BLOCK = 8192


def in_order(pieces, dim):
    pieces = jnp.moveaxis(pieces, 0, dim)
    shape = pieces.shape
    return pieces.reshape(*shape[:dim], shape[dim] * shape[dim + 1], *shape[dim + 2 :])


def from_everyone(value, axis):
    copies = jnp.broadcast_to(value, (lax.axis_size(axis), *value.shape))
    return lax.all_to_all(copies, axis, split_axis=0, concat_axis=0, tiled=True)


def gathered_copies(value, axis, dim):
    return in_order(from_everyone(value, axis), dim)


def from_behind(value, axis, steps):
    count = lax.axis_size(axis)
    first, last = (max(0, -steps), min(count, count - steps))
    return lax.ppermute(value, axis, [(source, source + steps) for source in range(first, last)])


def split_up(value, dim, count):
    before, after = (value.shape[:dim], value.shape[dim + 1 :])
    return jnp.moveaxis(value.reshape(*before, count, -1, *after), dim, 0)


def sum_at_owner(value, axis, dim):
    pieces = split_up(value, dim, lax.axis_size(axis))
    arrived = lax.all_to_all(pieces, axis, split_axis=0, concat_axis=0, tiled=True)
    return arrived.sum(axis=0)


def toeplitz_rows(segment, height, breadth):
    length = height + breadth - 1
    repeated = jnp.tile(segment, (1, height + 1))[:, : height * (length + 1)]
    return repeated.reshape(2, height, length + 1)[:, :, :breadth]


def mix_rows(samples, sample_index, doppler, window):
    phase_step = jnp.mod(doppler[:, None] * sample_index[None, :], window)
    phase_angle = phase_step.astype(jnp.float32) * (2.0 * math.pi / window)
    cosine = jnp.cos(phase_angle)
    sine_part = jnp.sin(phase_angle)
    real_in = samples[0].astype(jnp.float32)[None, :]
    imag_in = samples[1].astype(jnp.float32)[None, :]
    mixed_real = (real_in * cosine + imag_in * sine_part).astype(jnp.bfloat16)
    mixed_imag = (imag_in * cosine - real_in * sine_part).astype(jnp.bfloat16)
    upper_half = jnp.concatenate([mixed_real, mixed_imag], 1)
    lower_half = jnp.concatenate([mixed_imag, -mixed_real], 1)
    return jnp.concatenate([upper_half, lower_half], 0)


def lag_product(toeplitz, mixed):
    height = toeplitz.shape[1]
    stacked = toeplitz.reshape(2 * height, toeplitz.shape[2])
    return lax.dot_general(
        stacked, mixed, (((0,), (1,)), ((), ())), preferred_element_type=jnp.float32
    )


def on_device(surveillance, reference_signal):
    pieces = surveillance.shape[2]
    blocks_here = surveillance.shape[1]
    time_devices = lax.axis_size("tm")
    window = BLOCK * blocks_here * time_devices
    lag_rows = LAGS // time_devices
    full_block = gathered_copies(reference_signal, "dop", 2)
    bin_count = F
    row_shift = lax.axis_index("dop") * pieces
    block_tail = full_block[:, -1, BLOCK - LAGS + 1 :]
    earlier = from_behind(block_tail, "tm", 1)
    earlier_tails = jnp.concatenate(
        [earlier[:, None, :], full_block[:, :-1, BLOCK - LAGS + 1 :]], 1
    )
    extended = jnp.concatenate([earlier_tails, full_block], 2)
    row_count = surveillance.shape[2]
    height = min(512, row_count)
    sub_count = row_count // height
    doppler = jnp.arange(bin_count, dtype=jnp.int32) - F // 2
    block_start = lax.axis_index("tm") * blocks_here

    def one_turn(turn_no, running):
        block_no = turn_no // sub_count
        inside = turn_no % sub_count * height
        offset = row_shift + inside
        ext_row = lax.dynamic_index_in_dim(extended, block_no, 1, keepdims=False)
        segment = lax.dynamic_slice_in_dim(
            ext_row, offset, height + lag_rows * lax.axis_size("tm") - 1, 1
        )[:, ::-1]
        toeplitz = toeplitz_rows(segment, height, lag_rows * lax.axis_size("tm"))
        signal_row = lax.dynamic_index_in_dim(surveillance, block_no, 1, keepdims=False)
        samples = lax.dynamic_slice_in_dim(signal_row, inside, height, 1)[:, ::-1]
        sample_index = (
            (block_start + block_no) * BLOCK
            + offset
            + height
            - 1
            - jnp.arange(height, dtype=jnp.int32)
        )
        return running + lag_product(toeplitz, mix_rows(samples, sample_index, doppler, window))

    partial_value = lax.psum_scatter(
        lax.fori_loop(
            0,
            blocks_here * sub_count,
            one_turn,
            jnp.zeros((lag_rows * lax.axis_size("tm"), 2 * bin_count), jnp.float32),
        ),
        "tm",
        scatter_dimension=0,
        tiled=True,
    )
    result = sum_at_owner(partial_value.reshape(lag_rows, 2, F), "dop", 2)
    return result * (1.0 / math.sqrt(window))


def solution(mesh):
    return jax.shard_map(
        on_device,
        mesh=mesh,
        in_specs=(P(None, "tm", "dop"), P(None, "tm", "dop")),
        out_specs=P("tm", None, "dop"),
        check_vma=False,
    )
```

profile of v0, /device:TPU:1, one launch (start us, length us, event | category | flops | bytes accessed | tf_op | source)
XLA Modules:
  0.0 553.9 jit_solution(13793709630024011092)
XLA Ops:
  6.5 0.0 reduce-scatter.2.cloned.1.call-start
  6.5 0.7 broadcast_in_dim.22
  7.2 12.2 %all_to_all.10 = bf16[8,2,1,1024]{3,1,2,0:T(2,128)(2,1)S(1)} all-to-all(bf16[8,2,1,1024]{3,1,2,0:T(2,128)(2,1)S(1)} %broadcast_in_dim.22), channel_id=1, replica_groups=mesh['dop'=8,'tm'=32] {'dop'}, dimensions={0} | all-to-all | bytes 65536 | tf_op jit(solution)/shard_map/all_to_all | solution.py:21
  19.4 0.1 slice_bitcast_fusion
  19.5 6.1 %collective-permute-start = (bf16[2,2047]{1,0:T(2,128)(2,1)S(1)}, bf16[2,2047]{1,0:T(2,128)(2,1)S(1)}, u32[]{:S(2)}, u32[]{:S(2)}) collective-permute-start(bf16[2,2047]{1,0:T(2,128)(2,1)S(1)} %slice_bitcast_fusion), channel_id=1, source_target_pairs={{0,1},{1,2},{2,3},{3,4},{4,5},{5,6},{6,7},{7,8},{8,9},{9,10},{10,1... | collective-permute-start | bytes 24572 | tf_op jit(solution)/shard_map/ppermute | solution.py:31
  25.6 0.8 collective-permute-done
  26.4 0.1 pad_maximum_fusion
  26.5 114.1 %while.19 = (s32[]{:T(128)}, f32[2048,1024]{1,0:T(8,128)}, s32[]{:T(128)}, bf16[2,1,10239]{2,0,1:T(2,128)(2,1)S(1)}, bf16[2,1,1024]{2,0,1:T(2,128)(2,1)}, /*inde...) while((s32[]{:T(128)}, f32[2048,1024]{1,0:T(8,128)}, ...), condition=%wide.region_1.2_spmd.clone, body=%wide.region_0.1_spmd.clone.sunk | while | flops 4318824448 | bytes 85098944 | solution.py:115
  26.5 0.1 dynamic-slice_bitcast_fusion.5
  26.6 1.8 reverse.22
  28.4 0.1 slice.90
  28.5 2.8 tile.32
  31.3 12.7 %reshape.84 = bf16[2625534]{0:T(1024)(128)(2,1)} reshape(bf16[2,513,2559]{2,1,0:T(8,128)(2,1)} %tile.32) | data formatting | bytes 10502136 | tf_op jit(solution)/shard_map/while
  43.9 7.6 %tile.33 = bf16[2,1312767]{1,0:T(2,128)(2,1)} reshape(bf16[2625534]{0:T(1024)(128)(2,1)} %reshape.84) | data formatting | bytes 10502136 | tf_op jit(solution)/shard_map/while/body/eval_jaxpr/tile | solution.py:47
  51.6 0.0 slice-start
  51.6 2.5 slice-done
  54.0 0.8 copy.9
  54.8 0.0 copy-start
  54.9 2.6 slice.92
  57.5 0.0 copy-done
  57.5 0.1 dynamic-slice_bitcast_fusion.6
  57.5 0.4 slice.93
  57.9 0.4 slice.94
  58.3 4.7 add_convert_fusion.2
  63.0 4.7 fusion.22
  67.7 15.2 %select_add_fusion.2 = f32[2048,1024]{1,0:T(8,128)} fusion(f32[2048,1024]{1,0:T(8,128)} %get-tuple-element.376, pred[]{:T(512)S(6)} %compare.25, bf16[1024,2048]{1,0:T(8,128)(2,1)} %bitcast.43, bf16[512,512]{1,0:T(8,128)(2,1)S(1)} %fusion.22, bf16[512,512]{1,0:T(8,128)(2,1)S(1)} %get-tuple-element.357, bf16[512,512]{1,0:T(8,128)(2,1)S(1)} %get-tuple-element.358), kind=kOutput, calls=%fused_computation.1.clone.1 | convolution fusion | flops 4307550208 | bytes 22544384 | tf_op jit(solution)/shard_map/while/body/eval_jaxpr/dot_general | solution.py:68
  82.9 0.1 dynamic-slice_bitcast_fusion.5
  83.0 1.8 reverse.22
  84.8 0.1 slice.90
  84.9 2.8 tile.32
  87.7 12.7 %reshape.84 = bf16[2625534]{0:T(1024)(128)(2,1)} reshape(bf16[2,513,2559]{2,1,0:T(8,128)(2,1)} %tile.32) | data formatting | bytes 10502136 | tf_op jit(solution)/shard_map/while
  100.4 7.6 %tile.33 = bf16[2,1312767]{1,0:T(2,128)(2,1)} reshape(bf16[2625534]{0:T(1024)(128)(2,1)} %reshape.84) | data formatting | bytes 10502136 | tf_op jit(solution)/shard_map/while/body/eval_jaxpr/tile | solution.py:47
  108.0 0.0 slice-start
  108.0 2.5 slice-done
  110.4 0.8 copy.9
  111.2 0.0 copy-start
  111.3 2.6 slice.92
  113.9 0.0 copy-done
  113.9 0.1 dynamic-slice_bitcast_fusion.6
  113.9 0.4 slice.93
  114.3 0.4 slice.94
  114.7 4.7 add_convert_fusion.2
  119.4 4.7 fusion.22
  124.1 16.5 %select_add_fusion.2 = f32[2048,1024]{1,0:T(8,128)} fusion(f32[2048,1024]{1,0:T(8,128)} %get-tuple-element.376, pred[]{:T(512)S(6)} %compare.25, bf16[1024,2048]{1,0:T(8,128)(2,1)} %bitcast.43, bf16[512,512]{1,0:T(8,128)(2,1)S(1)} %fusion.22, bf16[512,512]{1,0:T(8,128)(2,1)S(1)} %get-tuple-element.357, bf16[512,512]{1,0:T(8,128)(2,1)S(1)} %get-tuple-element.358), kind=kOutput, calls=%fused_computation.1.clone.1 | convolution fusion | flops 4307550208 | bytes 22544384 | tf_op jit(solution)/shard_map/while/body/eval_jaxpr/dot_general | solution.py:68
  140.6 0.0 reduce-scatter.2.cloned.1.call-update
  140.6 384.1 %reduce-scatter.2.cloned.1.call-done = f32[64,1024]{1,0:T(8,128)} async-done(((f32[2048,1024]{1,0:T(8,128)}), f32[64,1024]{1,0:T(8,128)}) %reduce-scatter.2.cloned.1.call-update) | async-done | bytes 262160 | tf_op jit(solution)/shard_map/reduce_scatter | solution.py:114
  524.7 1.1 reshape_reshape.3
  525.8 0.3 copy.4
  526.1 0.6 reshape.81
  526.6 17.3 %all_to_all.11 = f32[8,1,8192]{2,1,0:T(1,128)S(1)} all-to-all(f32[8,1,8192]{2,1,0:T(1,128)S(1)} %reshape.81), channel_id=1, replica_groups=mesh['dop'=8,'tm'=32] {'dop'}, dimensions={0} | all-to-all | bytes 524288 | tf_op jit(solution)/shard_map/all_to_all | solution.py:41
  544.0 0.5 broadcast.113
  544.5 1.3 reduce
  545.7 0.4 reshape.82
  546.1 0.3 reduce_sum.9
  546.4 0.7 broadcast_multiply_fusion
  (7 shorter events, 0.0 us)
Async XLA Ops:
  6.5 518.2 %reduce-scatter.2.cloned.1.call-start = ((), (), s32[]{:S(2)}) async-start(), calls=%async_computation.3 | async-start | bytes 8650752 | tf_op jit(solution)/shard_map/reduce_scatter | solution.py:114
  19.5 6.9 %collective-permute-start = (bf16[2,2047]{1,0:T(2,128)(2,1)S(1)}, bf16[2,2047]{1,0:T(2,128)(2,1)S(1)}, u32[]{:S(2)}, u32[]{:S(2)}) collective-permute-start(bf16[2,2047]{1,0:T(2,128)(2,1)S(1)} %slice_bitcast_fusion), channel_id=1, source_target_pairs={{0,1},{1,2},{2,3},{3,4},{4,5},{5,6},{6,7},{7,8},{8,9},{9,10},{10,1... | collective-permute-start | bytes 24572 | tf_op jit(solution)/shard_map/ppermute | solution.py:31
  51.6 2.5 slice-start
  54.8 2.6 copy-start
  108.0 2.5 slice-start
  111.2 2.6 copy-start
Sparse Core Ops, SparseCore 0:
  140.7 383.9 reduce-scatter.1
where the time goes:
time: 554 us
  waiting for transfers between devices  385 us (69%)
  local copies, waits for them, and re-layouts  67 us (12%)
  matrix products  31.7 us (6%)
  blocking collectives  29.5 us (5%)
  other arithmetic  21.1 us (4%)
  between operations  13.5 us (2%)
  starting transfers between devices  6.12 us (1%)
    reduce_scatter x1, waiting for transfers between devices, on_device(): lax.psum_scatter(lax.fori_loop(0, blocks_here * sub_count, one_turn, jnp....  384 us
    dot_general x2, matrix products, lag_product(): lax.dot_general(stacked, mixed, (((0,), (1,)), ((), ())), preferred_eleme...  31.7 us
    while x12, local copies, waits for them, and re-layouts  30.8 us
    another operation x4, local copies, waits for them, and re-layouts, toeplitz_rows(): repeated = jnp.tile(segment, (1, height + 1))[:, :height * (length + 1)]  20.7 us
    all_to_all x1, blocking collectives, sum_at_owner(): lax.all_to_all(pieces, axis, split_axis=0, concat_axis=0, tiled=True)  17.3 us
    all_to_all x1, blocking collectives, from_everyone(): return lax.all_to_all(copies, axis, split_axis=0, concat_axis=0, tiled=True)  12.2 us
  transfers between devices with their start and end apart: 2, of which 2 were waited for; matrix products, arithmetic and copies ran while one was open for 0% of the time, Pallas kernels for 0%

commit v1 on v0

v1 whole, which is shorter than its diff:
```python
import functools
import math

import jax
import jax.numpy as jnp
import numpy as np
from jax import lax
from jax.experimental import pallas as pl
from jax.experimental.pallas import tpu as pltpu
from jax.sharding import PartitionSpec as P

MESH = pl.DeviceIdType.MESH
LANES = 128


class Plan:
    def __init__(self, mesh, samples_here, lags, bins, side_y=4, side_x=4):
        self.dop = mesh.shape["dop"]
        self.tm = mesh.shape["tm"]
        self.side_y, self.side_x = side_y, side_x
        self.columns = self.tm // 2
        self.zl_count = self.dop // 2
        self.slice = samples_here
        self.block = samples_here * self.dop
        self.window = self.block * self.tm
        self.lags = lags
        self.bins = bins
        self.own_lags = lags // self.tm
        self.own_bins = bins // self.dop
        self.pair_bins = 2 * self.own_bins
        self.tails = -(-lags // samples_here)
        assert 2 * self.own_lags == LANES and self.pair_bins == LANES
        assert self.columns == side_y * side_x
        self.slot_count = self.tails + self.dop
        offsets = [(dy, dx) for dy in range(side_y) for dx in range(side_x)]

        def hops(o):
            return min(o[0], side_y - o[0]) + min(o[1], side_x - o[1])

        self.offsets = sorted(offsets, key=lambda o: -hops(o))
        self.zs = 2 * self.zl_count


def phase_tables(plan):
    def turn(m):
        angle = (m % plan.window) * (2.0 * np.pi / plan.window)
        return np.stack([np.cos(angle), -np.sin(angle)]).astype(np.float32)

    j = np.arange(plan.pair_bins, dtype=np.int64)
    b = np.arange(plan.slice, dtype=np.int64)
    starts = np.arange(plan.dop * plan.tm, dtype=np.int64) * plan.slice
    near = turn(j[:, None] * b[None, :])
    far, low = [], []
    for zl in range(plan.zl_count):
        q0 = plan.pair_bins * zl - plan.bins // 2
        far.append(turn((q0 + j)[:, None] * starts[None, :]))
        low.append(turn(q0 * b))
    far = np.stack(far)
    pad = -far.shape[-1] % LANES
    far = np.pad(far, ((0, 0), (0, 0), (0, 0), (0, pad)))
    return near, far, np.stack(low)


def kernel(
    plan,
    s_hbm, r_hbm, near_hbm, far_hbm, low_hbm,
    out_ref,
    sown, rown, own, slots, near, far, low, ere, eim, x, toep, outbox, inbox, kept,
    load_sem, table_sem, s_send, t_send, s_recv, p_send, p_recv,
):
    c = plan
    t, d = lax.axis_index("tm"), lax.axis_index("dop")
    column, zh = t // 2, lax.rem(t, 2)
    zl, core = d // 2, lax.rem(d, 2)
    y, xx = column // c.side_x, lax.rem(column, c.side_x)
    block = 2 * column + core

    loads = [
        pltpu.make_async_copy(s_hbm, sown, load_sem.at[0]),
        pltpu.make_async_copy(r_hbm, rown, load_sem.at[1]),
    ]
    tables = [
        pltpu.make_async_copy(near_hbm, near, table_sem.at[0]),
        pltpu.make_async_copy(far_hbm.at[zl], far, table_sem.at[1]),
        pltpu.make_async_copy(low_hbm.at[zl], low, table_sem.at[2]),
    ]
    for copy in loads + tables:
        copy.start()

    barrier = pltpu.get_barrier_semaphore()

    def at(tm, dop):
        return {"tm": tm, "dop": dop}

    def greet(tm, dop):
        pl.semaphore_signal(barrier, inc=1, device_id=at(tm, dop), device_id_type=MESH)

    for other_zh in range(2):
        for other_d in range(c.dop):
            @pl.when(jnp.logical_or(other_zh != zh, other_d != d))
            def _():
                greet(2 * column + other_zh, other_d)

    def owner(offset):
        return lax.rem(y + offset[0], c.side_y) * c.side_x + lax.rem(xx + offset[1], c.side_x)

    for offset in c.offsets:
        if offset != (0, 0):
            for other_core in range(2):
                greet(2 * owner(offset) + zh, 2 * zl + other_core)

    @pl.when(jnp.logical_and(core == 0, column > 0))
    def _():
        for k in range(c.tails):
            greet(t - zh - 1, c.dop - c.tails + k)

    for copy in loads:
        copy.wait()
    own[0:2] = sown[:, 0]
    own[2:4] = rown[:, 0]

    sends_next = jnp.logical_and(zh == 1, jnp.logical_and(d >= c.dop - c.tails, column < c.columns - 1))
    peers = 2 * c.dop - 1 + 2 * (c.columns - 1)
    pl.semaphore_wait(barrier, peers + jnp.where(sends_next, c.zs, 0))

    def slice_copy(k):
        to = at(2 * column + k // c.zl_count, 2 * (k % c.zl_count) + zh)
        return pltpu.make_async_remote_copy(
            src_ref=own, dst_ref=slots.at[c.tails + d], send_sem=s_send.at[k],
            recv_sem=s_recv.at[c.tails + d], device_id=to, device_id_type=MESH)

    def is_me(k, tm, dop_core):
        return jnp.logical_and(
            jnp.logical_and(tm == column, k == zh * c.zl_count + zl), dop_core == core)

    next_block = t + 1
    next_column, next_core = next_block // 2, lax.rem(next_block, 2)
    sends_tail = jnp.logical_and(d >= c.dop - c.tails, next_block < c.tm)
    tail_slot = jnp.maximum(d - (c.dop - c.tails), 0)

    def tail_copy(k):
        to = at(2 * next_column + k // c.zl_count, 2 * (k % c.zl_count) + next_core)
        return pltpu.make_async_remote_copy(
            src_ref=own, dst_ref=slots.at[tail_slot], send_sem=t_send.at[k],
            recv_sem=s_recv.at[tail_slot], device_id=to, device_id_type=MESH)

    for k in range(c.zs):
        @pl.when(jnp.logical_not(is_me(k, column, zh)))
        def _():
            slice_copy(k).start()

        @pl.when(jnp.logical_and(sends_tail, jnp.logical_not(is_me(k, next_column, next_core))))
        def _():
            tail_copy(k).start()

    @pl.when(core == zh)
    def _():
        pltpu.make_async_copy(own, slots.at[c.tails + d], s_recv.at[c.tails + d]).start()

    self_tail = jnp.logical_and(sends_tail, jnp.logical_and(next_column == column, next_core == core))

    @pl.when(self_tail)
    def _():
        pltpu.make_async_copy(own, slots.at[tail_slot], s_recv.at[tail_slot]).start()

    @pl.when(block == 0)
    def _():
        slots[: c.tails] = jnp.zeros((c.tails, 4, c.slice), jnp.bfloat16)

    for copy in tables:
        copy.wait()
    far_lanes = far.shape[-1]

    def phases(k, carry):
        m = block * c.dop + k
        shift = lax.rem(far_lanes - m, far_lanes)
        cre = pltpu.roll(far[0], shift, 1)[:, :1]
        cim = pltpu.roll(far[1], shift, 1)[:, :1]
        for half in range(c.pair_bins // 32):
            rows = slice(half * 32, half * 32 + 32)
            for lane in range(0, c.slice, 256):
                nre, nim = near[0, rows, lane : lane + 256], near[1, rows, lane : lane + 256]
                where = pl.ds(pl.multiple_of(k * c.slice + lane, LANES), 256)
                ere[rows, where] = cre[rows] * nre - cim[rows] * nim
                eim[rows, where] = cre[rows] * nim + cim[rows] * nre
        return carry

    lax.fori_loop(0, c.dop, phases, 0)

    for k in range(c.slot_count):
        def arrived():
            pltpu.make_async_copy(own, slots.at[k], s_recv.at[k]).wait()

        if k < c.tails:
            pl.when(block > 0)(arrived)
        else:
            arrived()

    wide = c.slice + LANES
    row = lax.broadcasted_iota(jnp.int32, (8, wide), 0)

    def shifts(slot, carry):
        both = slots[slot].astype(jnp.float32)
        before = slots[jnp.maximum(slot - 1, 0)].astype(jnp.float32)
        place = pl.ds(pl.multiple_of(slot * c.slice, LANES), c.slice)
        for part in (2, 3):
            line = jnp.concatenate(
                [before[part : part + 1, c.slice - LANES :], both[part : part + 1]], 1)
            base = jnp.broadcast_to(line, (8, wide))
            base = jnp.where(zh == 1, pltpu.roll(base, c.own_lags, 1), base)
            for step in (1, 2, 4):
                base = jnp.where(row & step != 0, pltpu.roll(base, step, 1), base)
            for high in range(0, c.own_lags, 16):
                pair = [
                    (pltpu.roll(base, at_row, 1) if at_row else base)[:, LANES:]
                    for at_row in (high, high + 8)
                ]
                top = (part - 2) * c.own_lags + high
                toep[top : top + 16, place] = jnp.concatenate(pair, 0).astype(jnp.bfloat16)
        return carry

    lax.fori_loop(0, c.slot_count, shifts, 0)

    def mixing(k, carry):
        both = slots[c.tails + k].astype(jnp.float32)
        lre, lim = low[0:1], low[1:2]
        sre = both[0:1] * lre - both[1:2] * lim
        sim = both[0:1] * lim + both[1:2] * lre
        for half in range(2):
            for sub in range(0, c.own_bins, 32):
                rows = slice(half * c.own_bins + sub, half * c.own_bins + sub + 32)
                top = 2 * half * c.own_bins + sub
                for lane in range(0, c.slice, 256):
                    where = pl.ds(pl.multiple_of(k * c.slice + lane, LANES), 256)
                    pre, pim = ere[rows, where], eim[rows, where]
                    are, aim = sre[:, lane : lane + 256], sim[:, lane : lane + 256]
                    x[top : top + 32, where] = (are * pre - aim * pim).astype(jnp.bfloat16)
                    low_rows = slice(top + c.own_bins, top + c.own_bins + 32)
                    x[low_rows, where] = (are * pim + aim * pre).astype(jnp.bfloat16)
        return carry

    lax.fori_loop(0, c.dop, mixing, 0)

    sign = jnp.where(lax.broadcasted_iota(jnp.int32, (1, LANES), 1) < c.own_bins, 1.0, -1.0)
    GROUP = 4

    def piece_copy(k, other_core):
        n = 2 * k + other_core
        return pltpu.make_async_remote_copy(
            src_ref=outbox.at[n], dst_ref=inbox.at[block], send_sem=p_send.at[n],
            recv_sem=p_recv.at[block],
            device_id=at(2 * owner(c.offsets[k]) + zh, 2 * zl + other_core), device_id_type=MESH)

    for first in range(0, c.columns, GROUP):
        members = range(first, min(first + GROUP, c.columns))
        windows = []
        for k in members:
            start = pl.multiple_of(c.tails * c.slice - LANES * owner(c.offsets[k]), LANES)
            windows.append(toep[:, pl.ds(start, c.block)])
        product = lax.dot_general(
            jnp.concatenate(windows, 0), x[...], (((1,), (1,)), ((), ())),
            preferred_element_type=jnp.float32)
        for at_row, k in enumerate(members):
            top = at_row * 2 * c.own_lags
            for other_core in range(2):
                cols = slice(other_core * LANES, (other_core + 1) * LANES)
                a = product[top : top + c.own_lags, cols]
                b = product[top + c.own_lags : top + 2 * c.own_lags, cols]
                piece = a + pltpu.roll(b, c.own_bins, 1) * sign
                if c.offsets[k] == (0, 0):
                    @pl.when(core == other_core)
                    def _():
                        kept[...] = piece

                    outbox[2 * k + other_core] = piece.astype(jnp.bfloat16)

                    @pl.when(core != other_core)
                    def _():
                        piece_copy(k, other_core).start()
                else:
                    outbox[2 * k + other_core] = piece.astype(jnp.bfloat16)
                    piece_copy(k, other_core).start()

    total = kept[...]

    def add(n, total):
        @pl.when(n != block)
        def _():
            pltpu.make_async_copy(outbox.at[0], inbox.at[n], p_recv.at[n]).wait()

        return total + jnp.where(n == block, 0.0, inbox[n].astype(jnp.float32))

    @pl.when(True)
    def _():
        inbox[block] = jnp.zeros((c.own_lags, LANES), jnp.bfloat16)

    total = lax.fori_loop(0, c.tm, add, total) * (1.0 / math.sqrt(c.window))
    out_ref[:, 0, :] = total[:, : c.own_bins]
    out_ref[:, 1, :] = total[:, c.own_bins :]

    for k in range(c.zs):
        @pl.when(jnp.logical_not(is_me(k, column, zh)))
        def _():
            slice_copy(k).wait_send()

        @pl.when(jnp.logical_and(sends_tail, jnp.logical_not(is_me(k, next_column, next_core))))
        def _():
            tail_copy(k).wait_send()

    for k in range(c.columns):
        for other_core in range(2):
            if c.offsets[k] == (0, 0):
                @pl.when(core != other_core)
                def _():
                    piece_copy(k, other_core).wait_send()
            else:
                piece_copy(k, other_core).wait_send()


def run(plan, surveillance, reference_signal):
    c = plan
    near, far, low = phase_tables(c)
    f32, bf16 = jnp.float32, jnp.bfloat16
    anywhere = pl.BlockSpec(memory_space=pl.ANY)
    dma = pltpu.SemaphoreType.DMA
    return pl.pallas_call(
        functools.partial(kernel, c),
        out_shape=jax.ShapeDtypeStruct((c.own_lags, 2, c.own_bins), f32),
        in_specs=[anywhere] * 5,
        out_specs=pl.BlockSpec(memory_space=pltpu.VMEM),
        scratch_shapes=[
            pltpu.VMEM((2, 1, c.slice), bf16),
            pltpu.VMEM((2, 1, c.slice), bf16),
            pltpu.VMEM((4, c.slice), bf16),
            pltpu.VMEM((c.slot_count, 4, c.slice), bf16),
            pltpu.VMEM(near.shape, f32),
            pltpu.VMEM(far.shape[1:], f32),
            pltpu.VMEM(low.shape[1:], f32),
            pltpu.VMEM((c.pair_bins, c.block), f32),
            pltpu.VMEM((c.pair_bins, c.block), f32),
            pltpu.VMEM((2 * c.pair_bins, c.block), bf16),
            pltpu.VMEM((2 * c.own_lags, c.slot_count * c.slice), bf16),
            pltpu.VMEM((2 * c.columns, c.own_lags, LANES), bf16),
            pltpu.VMEM((c.tm, c.own_lags, LANES), bf16),
            pltpu.VMEM((c.own_lags, LANES), f32),
            dma((2,)), dma((3,)), dma((c.zs,)), dma((c.zs,)),
            dma((c.slot_count,)), dma((2 * c.columns,)), dma((c.tm,)),
        ],
        compiler_params=pltpu.CompilerParams(
            collective_id=0, has_side_effects=True, vmem_limit_bytes=60 * 1024 * 1024),
    )(surveillance, reference_signal, jnp.asarray(near), jnp.asarray(far), jnp.asarray(low))


def solution(mesh, lags=2048, bins=512, side_y=4, side_x=4):
    def on_device(surveillance, reference_signal):
        plan = Plan(mesh, surveillance.shape[2], lags, bins, side_y, side_x)
        return run(plan, surveillance, reference_signal)

    return jax.shard_map(
        on_device,
        mesh=mesh,
        in_specs=(P(None, "tm", "dop"), P(None, "tm", "dop")),
        out_specs=P("tm", None, "dop"),
        check_vma=False,
    )
```

time: 554 us -> 48.2 us (0.09)
  waiting for transfers between devices: 385 us -> 0 us
  local copies, waits for them, and re-layouts: 67 us -> 3.38 us
  Pallas kernels: 0 us -> 44.7 us
  matrix products: 31.7 us -> 0 us
  blocking collectives: 29.5 us -> 0 us
  other arithmetic: 21.1 us -> 0 us
  between operations: 13.5 us -> 0.01 us
  starting transfers between devices: 6.12 us -> 0 us
    reduce_scatter x1 -> x0, waiting for transfers between devices: 384 us -> none  [on_device(): lax.psum_scatter(lax.fori_loop(0, blocks_here * sub_count, one_turn, jnp....]
    pallas_call x0 -> x1, Pallas kernels: none -> 44.7 us  [run(): pl.pallas_call(functools.partial(kernel, c), out_shape=jax.ShapeDtypeStru...]
    dot_general x2 -> x0, matrix products: 31.7 us -> none  [lag_product(): lax.dot_general(stacked, mixed, (((0,), (1,)), ((), ())), preferred_eleme...]
    while x12 -> x0, local copies, waits for them, and re-layouts: 30.8 us -> none
    all_to_all x2 -> x0, blocking collectives: 29.5 us -> none  [the longest x1 17.3 us: sum_at_owner(): lax.all_to_all(pieces, axis, split_axis=0, concat_axis=0, tiled=True)]
    another operation x5 -> x0, local copies, waits for them, and re-layouts: 21.8 us -> none  [the longest x4 20.7 us: toeplitz_rows(): repeated = jnp.tile(segment, (1, height + 1))[:, :height * (length + 1)]]
    slice x12 -> x0, local copies, waits for them, and re-layouts: 11.8 us -> none  [the longest x2 5.21 us: toeplitz_rows(): return repeated.reshape(2, height, length + 1)[:, :, :breadth]]
    convert_element_type x2 -> x0, other arithmetic: 9.49 us -> none  [mix_rows(): mixed_real = (real_in * cosine + imag_in * sine_part).astype(jnp.bfloat16)]
  transfers between devices with their start and end apart: 2 -> 0, of which waited for: 2 -> 0; matrix products, arithmetic and copies ran while one was open for 0% -> 0% of each run, Pallas kernels for 0% -> 0%
where the time goes in v1:
time: 48.2 us; the launch traced here: 48.1 us
  Pallas kernels  44.7 us (93%)
  local copies, waits for them, and re-layouts  3.38 us (7%)
    pallas_call x1, Pallas kernels, run(): pl.pallas_call(functools.partial(kernel, c), out_shape=jax.ShapeDtypeStru...  44.7 us
    unnamed x5, local copies, waits for them, and re-layouts  3.38 us

profile of v1, /device:TPU:1, one launch (start us, length us, event | category | flops | bytes accessed | tf_op | source)
XLA Modules:
  0.0 48.1 jit_solution(6180365085366974371)
XLA Ops:
  0.0 0.0 copy-start
  0.0 1.3 %copy.6.s_hbm = bf16[2,1,1024]{2,1,0:T(2,128)(2,1)} copy(bf16[2,1,1024]{2,0,1:T(2,128)(2,1)} %param.5) | data formatting | bytes 8192 | tf_op args[0]
  1.3 0.0 copy-done
  1.3 0.6 %copy.7.r_hbm = bf16[2,1,1024]{2,1,0:T(2,128)(2,1)} copy(bf16[2,1,1024]{2,0,1:T(2,128)(2,1)S(1)} %copy-done) | data formatting | bytes 8192 | tf_op args[1]
  1.9 44.7 %shard_map.55 = f32[64,2,64]{2,1,0:T(2,128)} custom-call(bf16[2,1,1024]{2,1,0:T(2,128)(2,1)} %copy.6.s_hbm, bf16[2,1,1024]{2,1,0:T(2,128)(2,1)} %copy.7.r_hbm, f32[2,128,1024]{2,1,0:T(8,128)} %constant.6.clone.near_hbm, f32[4,2,128,256]{3,2,1,0:T(8,128)} %constant.7.clone.far_hbm, f32[4,2,1024]{2,1,0:T(2,128)} %constant.8.clone.low_hbm), custom_call_target="tpu_custom_call" | custom-call | tf_op jit(solution)/shard_map/pallas_call | solution.py:326
  46.6 1.5 %copy.9 = f32[64,2,64]{2,1,0:T(2,128)} copy(f32[64,2,64]{2,1,0:T(2,128)} %shard_map.55) | data formatting | bytes 65536
Async XLA Ops:
  0.0 1.3 %copy-start = (bf16[2,1,1024]{2,0,1:T(2,128)(2,1)S(1)}, bf16[2,1,1024]{2,0,1:T(2,128)(2,1)}, u32[]{:S(2)}) copy-start(bf16[2,1,1024]{2,0,1:T(2,128)(2,1)} %param.6) | copy-start | bytes 12292

commit v2 on v1

--- a/solution.py
+++ b/solution.py
@@ -11,6 +11,7 @@
 
 MESH = pl.DeviceIdType.MESH
 LANES = 128
+GROUP = 4
 
 
 class Plan:
@@ -116,8 +117,8 @@
 
     for copy in loads:
         copy.wait()
-    own[0:2] = sown[:, 0]
-    own[2:4] = rown[:, 0]
+    own[0:2] = sown[...]
+    own[2:4] = rown[...]
 
     sends_next = jnp.logical_and(zh == 1, jnp.logical_and(d >= c.dop - c.tails, column < c.columns - 1))
     peers = 2 * c.dop - 1 + 2 * (c.columns - 1)
@@ -242,59 +243,72 @@
     lax.fori_loop(0, c.dop, mixing, 0)
 
     sign = jnp.where(lax.broadcasted_iota(jnp.int32, (1, LANES), 1) < c.own_bins, 1.0, -1.0)
-    GROUP = 4
-
-    def piece_copy(k, other_core):
-        n = 2 * k + other_core
+    members = min(GROUP, c.columns)
+    groups = c.columns // members
+
+    def offset_of(group, member):
+        def digit(axis, side):
+            code = sum(c.offsets[g * members + member][axis] * side**g for g in range(groups))
+            scale = 1
+            for g in range(1, groups):
+                scale = jnp.where(group == g, side**g, scale)
+            return lax.rem(code // scale, side)
+
+        return digit(0, c.side_y), digit(1, c.side_x)
+
+    def piece_copy(group, member, other_core):
+        n = 2 * (group * members + member) + other_core
         return pltpu.make_async_remote_copy(
             src_ref=outbox.at[n], dst_ref=inbox.at[block], send_sem=p_send.at[n],
             recv_sem=p_recv.at[block],
-            device_id=at(2 * owner(c.offsets[k]) + zh, 2 * zl + other_core), device_id_type=MESH)
-
-    for first in range(0, c.columns, GROUP):
-        members = range(first, min(first + GROUP, c.columns))
+            device_id=at(2 * owner(offset_of(group, member)) + zh, 2 * zl + other_core),
+            device_id_type=MESH)
+
+    def stays(group, member, other_core):
+        last = jnp.logical_and(group == groups - 1, core == other_core)
+        return last if member == members - 1 else False
+
+    def products(group, carry):
         windows = []
-        for k in members:
-            start = pl.multiple_of(c.tails * c.slice - LANES * owner(c.offsets[k]), LANES)
-            windows.append(toep[:, pl.ds(start, c.block)])
+        for member in range(members):
+            to = owner(offset_of(group, member))
+            windows.append(toep[:, pl.ds(pl.multiple_of(c.tails * c.slice - LANES * to, LANES), c.block)])
         product = lax.dot_general(
             jnp.concatenate(windows, 0), x[...], (((1,), (1,)), ((), ())),
             preferred_element_type=jnp.float32)
-        for at_row, k in enumerate(members):
-            top = at_row * 2 * c.own_lags
+        for member in range(members):
+            top = member * 2 * c.own_lags
             for other_core in range(2):
                 cols = slice(other_core * LANES, (other_core + 1) * LANES)
                 a = product[top : top + c.own_lags, cols]
                 b = product[top + c.own_lags : top + 2 * c.own_lags, cols]
                 piece = a + pltpu.roll(b, c.own_bins, 1) * sign
-                if c.offsets[k] == (0, 0):
-                    @pl.when(core == other_core)
+                outbox[2 * (group * members + member) + other_core] = piece.astype(jnp.bfloat16)
+                if member < members - 1:
+                    piece_copy(group, member, other_core).start()
+                else:
+                    here = stays(group, member, other_core)
+
+                    @pl.when(here)
                     def _():
                         kept[...] = piece
 
-                    outbox[2 * k + other_core] = piece.astype(jnp.bfloat16)
-
-                    @pl.when(core != other_core)
+                    @pl.when(jnp.logical_not(here))
                     def _():
-                        piece_copy(k, other_core).start()
-                else:
-                    outbox[2 * k + other_core] = piece.astype(jnp.bfloat16)
-                    piece_copy(k, other_core).start()
+                        piece_copy(group, member, other_core).start()
+        return carry
+
+    lax.fori_loop(0, groups, products, 0)
 
     total = kept[...]
-
-    def add(n, total):
-        @pl.when(n != block)
-        def _():
+    for offset in c.offsets:
+        source = lax.rem(y + c.side_y - offset[0], c.side_y) * c.side_x + lax.rem(
+            xx + c.side_x - offset[1], c.side_x)
+        for n in [2 * source + 1 - core] if offset == (0, 0) else [2 * source, 2 * source + 1]:
             pltpu.make_async_copy(outbox.at[0], inbox.at[n], p_recv.at[n]).wait()
-
-        return total + jnp.where(n == block, 0.0, inbox[n].astype(jnp.float32))
-
-    @pl.when(True)
-    def _():
-        inbox[block] = jnp.zeros((c.own_lags, LANES), jnp.bfloat16)
-
-    total = lax.fori_loop(0, c.tm, add, total) * (1.0 / math.sqrt(c.window))
+            total = total + inbox[n].astype(jnp.float32)
+
+    total = total * (1.0 / math.sqrt(c.window))
     out_ref[:, 0, :] = total[:, : c.own_bins]
     out_ref[:, 1, :] = total[:, c.own_bins :]
 
@@ -307,14 +321,15 @@
         def _():
             tail_copy(k).wait_send()
 
-    for k in range(c.columns):
-        for other_core in range(2):
-            if c.offsets[k] == (0, 0):
-                @pl.when(core != other_core)
+    def left(group, carry):
+        for member in range(members):
+            for other_core in range(2):
+                @pl.when(jnp.logical_not(stays(group, member, other_core)))
                 def _():
-                    piece_copy(k, other_core).wait_send()
-            else:
-                piece_copy(k, other_core).wait_send()
+                    piece_copy(group, member, other_core).wait_send()
+        return carry
+
+    lax.fori_loop(0, groups, left, 0)
 
 
 def run(plan, surveillance, reference_signal):
@@ -329,8 +344,8 @@
         in_specs=[anywhere] * 5,
         out_specs=pl.BlockSpec(memory_space=pltpu.VMEM),
         scratch_shapes=[
-            pltpu.VMEM((2, 1, c.slice), bf16),
-            pltpu.VMEM((2, 1, c.slice), bf16),
+            pltpu.VMEM((2, c.slice), bf16),
+            pltpu.VMEM((2, c.slice), bf16),
             pltpu.VMEM((4, c.slice), bf16),
             pltpu.VMEM((c.slot_count, 4, c.slice), bf16),
             pltpu.VMEM(near.shape, f32),
@@ -348,7 +363,7 @@
         ],
         compiler_params=pltpu.CompilerParams(
             collective_id=0, has_side_effects=True, vmem_limit_bytes=60 * 1024 * 1024),
-    )(surveillance, reference_signal, jnp.asarray(near), jnp.asarray(far), jnp.asarray(low))
+    )(surveillance.reshape(2, -1), reference_signal.reshape(2, -1), jnp.asarray(near), jnp.asarray(far), jnp.asarray(low))
 
 
 def solution(mesh, lags=2048, bins=512, side_y=4, side_x=4):

time: 48.2 us -> 38 us (0.79)
  Pallas kernels: 44.7 us -> 36.4 us
  local copies, waits for them, and re-layouts: 3.38 us -> 1.47 us
    pallas_call x1, Pallas kernels: 44.7 us -> 36.4 us  [run(): pl.pallas_call(functools.partial(kernel, c), out_shape=jax.ShapeDtypeStru...]
    unnamed x5 -> x1, local copies, waits for them, and re-layouts: 3.38 us -> 1.47 us
where the time goes in v2:
time: 38 us; the launch traced here: 37.9 us
  Pallas kernels  36.4 us (96%)
  local copies, waits for them, and re-layouts  1.47 us (4%)
    pallas_call x1, Pallas kernels, run(): pl.pallas_call(functools.partial(kernel, c), out_shape=jax.ShapeDtypeStru...  36.4 us
    unnamed x1, local copies, waits for them, and re-layouts  1.47 us

profile of v2, /device:TPU:1, one launch (start us, length us, event | category | flops | bytes accessed | tf_op | source)
XLA Modules:
  0.0 37.9 jit_solution(10038117916749318196)
XLA Ops:
  0.0 36.4 %shard_map.55 = f32[64,2,64]{2,1,0:T(2,128)} custom-call(bf16[2,1024]{1,0:T(2,128)(2,1)} %bitcast.2, bf16[2,1024]{1,0:T(2,128)(2,1)} %bitcast.3, f32[2,128,1024]{2,1,0:T(8,128)} %constant.6.clone.near_hbm, f32[4,2,128,256]{3,2,1,0:T(8,128)} %constant.7.clone.far_hbm, f32[4,2,1024]{2,1,0:T(2,128)} %constant.8.clone.low_hbm), custom_call_target="tpu_custom_call" | custom-call | tf_op jit(solution)/shard_map/pallas_call | solution.py:341
  36.4 1.5 %copy.7 = f32[64,2,64]{2,1,0:T(2,128)} copy(f32[64,2,64]{2,1,0:T(2,128)} %shard_map.55) | data formatting | bytes 65536

commit v3 on v2

--- a/solution.py
+++ b/solution.py
@@ -121,53 +121,6 @@
     own[2:4] = rown[...]
 
     sends_next = jnp.logical_and(zh == 1, jnp.logical_and(d >= c.dop - c.tails, column < c.columns - 1))
-    peers = 2 * c.dop - 1 + 2 * (c.columns - 1)
-    pl.semaphore_wait(barrier, peers + jnp.where(sends_next, c.zs, 0))
-
-    def slice_copy(k):
-        to = at(2 * column + k // c.zl_count, 2 * (k % c.zl_count) + zh)
-        return pltpu.make_async_remote_copy(
-            src_ref=own, dst_ref=slots.at[c.tails + d], send_sem=s_send.at[k],
-            recv_sem=s_recv.at[c.tails + d], device_id=to, device_id_type=MESH)
-
-    def is_me(k, tm, dop_core):
-        return jnp.logical_and(
-            jnp.logical_and(tm == column, k == zh * c.zl_count + zl), dop_core == core)
-
-    next_block = t + 1
-    next_column, next_core = next_block // 2, lax.rem(next_block, 2)
-    sends_tail = jnp.logical_and(d >= c.dop - c.tails, next_block < c.tm)
-    tail_slot = jnp.maximum(d - (c.dop - c.tails), 0)
-
-    def tail_copy(k):
-        to = at(2 * next_column + k // c.zl_count, 2 * (k % c.zl_count) + next_core)
-        return pltpu.make_async_remote_copy(
-            src_ref=own, dst_ref=slots.at[tail_slot], send_sem=t_send.at[k],
-            recv_sem=s_recv.at[tail_slot], device_id=to, device_id_type=MESH)
-
-    for k in range(c.zs):
-        @pl.when(jnp.logical_not(is_me(k, column, zh)))
-        def _():
-            slice_copy(k).start()
-
-        @pl.when(jnp.logical_and(sends_tail, jnp.logical_not(is_me(k, next_column, next_core))))
-        def _():
-            tail_copy(k).start()
-
-    @pl.when(core == zh)
-    def _():
-        pltpu.make_async_copy(own, slots.at[c.tails + d], s_recv.at[c.tails + d]).start()
-
-    self_tail = jnp.logical_and(sends_tail, jnp.logical_and(next_column == column, next_core == core))
-
-    @pl.when(self_tail)
-    def _():
-        pltpu.make_async_copy(own, slots.at[tail_slot], s_recv.at[tail_slot]).start()
-
-    @pl.when(block == 0)
-    def _():
-        slots[: c.tails] = jnp.zeros((c.tails, 4, c.slice), jnp.bfloat16)
-
     for copy in tables:
         copy.wait()
     far_lanes = far.shape[-1]
@@ -188,41 +141,85 @@
 
     lax.fori_loop(0, c.dop, phases, 0)
 
-    for k in range(c.slot_count):
-        def arrived():
-            pltpu.make_async_copy(own, slots.at[k], s_recv.at[k]).wait()
-
-        if k < c.tails:
-            pl.when(block > 0)(arrived)
-        else:
-            arrived()
-
-    wide = c.slice + LANES
-    row = lax.broadcasted_iota(jnp.int32, (8, wide), 0)
-
-    def shifts(slot, carry):
+    peers = 2 * c.dop - 1 + 2 * (c.columns - 1)
+    pl.semaphore_wait(barrier, peers + jnp.where(sends_next, c.zs, 0))
+
+    def slice_copy(k):
+        to = at(2 * column + k // c.zl_count, 2 * (k % c.zl_count) + zh)
+        return pltpu.make_async_remote_copy(
+            src_ref=own, dst_ref=slots.at[c.tails + d], send_sem=s_send.at[k],
+            recv_sem=s_recv.at[c.tails + d], device_id=to, device_id_type=MESH)
+
+    def is_me(k, tm, dop_core):
+        return jnp.logical_and(
+            jnp.logical_and(tm == column, k == zh * c.zl_count + zl), dop_core == core)
+
+    next_block = t + 1
+    next_column, next_core = next_block // 2, lax.rem(next_block, 2)
+    sends_tail = jnp.logical_and(d >= c.dop - c.tails, next_block < c.tm)
+    tail_slot = jnp.maximum(d - (c.dop - c.tails), 0)
+
+    def tail_copy(k):
+        to = at(2 * next_column + k // c.zl_count, 2 * (k % c.zl_count) + next_core)
+        return pltpu.make_async_remote_copy(
+            src_ref=own, dst_ref=slots.at[tail_slot], send_sem=t_send.at[k],
+            recv_sem=s_recv.at[tail_slot], device_id=to, device_id_type=MESH)
+
+    for k in range(c.zs):
+        @pl.when(jnp.logical_not(is_me(k, column, zh)))
+        def _():
+            slice_copy(k).start()
+
+        @pl.when(jnp.logical_and(sends_tail, jnp.logical_not(is_me(k, next_column, next_core))))
+        def _():
+            tail_copy(k).start()
+
+    @pl.when(core == zh)
+    def _():
+        pltpu.make_async_copy(own, slots.at[c.tails + d], s_recv.at[c.tails + d]).start()
+
+    self_tail = jnp.logical_and(sends_tail, jnp.logical_and(next_column == column, next_core == core))
+
+    @pl.when(self_tail)
+    def _():
+        pltpu.make_async_copy(own, slots.at[tail_slot], s_recv.at[tail_slot]).start()
+
+    @pl.when(block == 0)
+    def _():
+        slots[: c.tails] = jnp.zeros((c.tails, 4, c.slice), jnp.bfloat16)
+
+    lane_no = lax.broadcasted_iota(jnp.int32, (8, LANES), 1)
+    row_no = lax.broadcasted_iota(jnp.int32, (8, LANES), 0) + c.own_lags * zh
+    reach = [row_no + high for high in range(0, c.own_lags, 8)]
+    source_lane = [lax.rem(lane_no - shift + 2 * LANES, LANES) for shift in reach]
+    own_part = [lane_no >= shift for shift in reach]
+
+    def wait_slot(slot):
+        pltpu.make_async_copy(own, slots.at[slot], s_recv.at[slot]).wait()
+
+    def shifts(slot):
         both = slots[slot].astype(jnp.float32)
-        before = slots[jnp.maximum(slot - 1, 0)].astype(jnp.float32)
-        place = pl.ds(pl.multiple_of(slot * c.slice, LANES), c.slice)
         for part in (2, 3):
-            line = jnp.concatenate(
-                [before[part : part + 1, c.slice - LANES :], both[part : part + 1]], 1)
-            base = jnp.broadcast_to(line, (8, wide))
-            base = jnp.where(zh == 1, pltpu.roll(base, c.own_lags, 1), base)
-            for step in (1, 2, 4):
-                base = jnp.where(row & step != 0, pltpu.roll(base, step, 1), base)
             for high in range(0, c.own_lags, 16):
-                pair = [
-                    (pltpu.roll(base, at_row, 1) if at_row else base)[:, LANES:]
-                    for at_row in (high, high + 8)
-                ]
-                top = (part - 2) * c.own_lags + high
-                toep[top : top + 16, place] = jnp.concatenate(pair, 0).astype(jnp.bfloat16)
-        return carry
-
-    lax.fori_loop(0, c.slot_count, shifts, 0)
-
-    def mixing(k, carry):
+                groups = (high // 8, high // 8 + 1)
+                keep = jnp.concatenate([own_part[g] for g in groups], 0)
+                rows = slice((part - 2) * c.own_lags + high, (part - 2) * c.own_lags + high + 16)
+                last = None
+                for tile in range(c.slice // LANES + 1):
+                    place = pl.ds(pl.multiple_of(slot * c.slice + tile * LANES, LANES), LANES)
+                    if tile < c.slice // LANES:
+                        line = both[part : part + 1, tile * LANES : tile * LANES + LANES]
+                        wide = jnp.broadcast_to(line, (8, LANES))
+                        turned = jnp.concatenate(
+                            [jnp.take_along_axis(wide, source_lane[g], axis=1) for g in groups], 0)
+                    else:
+                        turned = toep[rows, place].astype(jnp.float32)
+                    if last is None:
+                        last = toep[rows, place].astype(jnp.float32)
+                    toep[rows, place] = jnp.where(keep, turned, last).astype(jnp.bfloat16)
+                    last = turned
+
+    def mixing(k):
         both = slots[c.tails + k].astype(jnp.float32)
         lre, lim = low[0:1], low[1:2]
         sre = both[0:1] * lre - both[1:2] * lim
@@ -238,9 +235,30 @@
                     x[top : top + 32, where] = (are * pre - aim * pim).astype(jnp.bfloat16)
                     low_rows = slice(top + c.own_bins, top + c.own_bins + 32)
                     x[low_rows, where] = (are * pim + aim * pre).astype(jnp.bfloat16)
-        return carry
-
-    lax.fori_loop(0, c.dop, mixing, 0)
+
+    def arrival(n, carry):
+        place, core_there = n // 2, lax.rem(n, 2)
+        place = jnp.where(zh == core, place, c.zl_count - 1 - place)
+        flipped = lax.rem(zl // 2 + place // 2, 2) * 2 + lax.rem(zl + place, 2)
+        there = flipped if c.zl_count == 4 else place
+        k = 2 * there + core_there
+        wait_slot(c.tails + k)
+        mixing(k)
+        shifts(c.tails + k)
+        return carry
+
+    lax.fori_loop(0, c.dop, arrival, 0)
+
+    @pl.when(block > 0)
+    def _():
+        for k in range(c.tails):
+            wait_slot(k)
+
+    def tail_shifts(slot, carry):
+        shifts(slot)
+        return carry
+
+    lax.fori_loop(0, c.tails, tail_shifts, 0)
 
     sign = jnp.where(lax.broadcasted_iota(jnp.int32, (1, LANES), 1) < c.own_bins, 1.0, -1.0)
     members = min(GROUP, c.columns)
@@ -354,7 +372,7 @@
             pltpu.VMEM((c.pair_bins, c.block), f32),
             pltpu.VMEM((c.pair_bins, c.block), f32),
             pltpu.VMEM((2 * c.pair_bins, c.block), bf16),
-            pltpu.VMEM((2 * c.own_lags, c.slot_count * c.slice), bf16),
+            pltpu.VMEM((2 * c.own_lags, c.slot_count * c.slice + LANES), bf16),
             pltpu.VMEM((2 * c.columns, c.own_lags, LANES), bf16),
             pltpu.VMEM((c.tm, c.own_lags, LANES), bf16),
             pltpu.VMEM((c.own_lags, LANES), f32),

time: 38 us -> 33.7 us (0.89)
  Pallas kernels: 36.4 us -> 32 us
    pallas_call x1, Pallas kernels: 36.4 us -> 32 us  [run(): pl.pallas_call(functools.partial(kernel, c), out_shape=jax.ShapeDtypeStru...]
where the time goes in v3:
time: 33.7 us; the launch traced here: 33.5 us
  Pallas kernels  32 us (95%)
  local copies, waits for them, and re-layouts  1.47 us (4%)
    pallas_call x1, Pallas kernels, run(): pl.pallas_call(functools.partial(kernel, c), out_shape=jax.ShapeDtypeStru...  32 us
    unnamed x1, local copies, waits for them, and re-layouts  1.47 us

profile of v3, /device:TPU:1, one launch (start us, length us, event | category | flops | bytes accessed | tf_op | source)
XLA Modules:
  0.0 33.5 jit_solution(16833890950150712967)
XLA Ops:
  0.0 32.0 %shard_map.55 = f32[64,2,64]{2,1,0:T(2,128)} custom-call(bf16[2,1024]{1,0:T(2,128)(2,1)} %bitcast.2, bf16[2,1024]{1,0:T(2,128)(2,1)} %bitcast.3, f32[2,128,1024]{2,1,0:T(8,128)} %constant.6.clone.near_hbm, f32[4,2,128,256]{3,2,1,0:T(8,128)} %constant.7.clone.far_hbm, f32[4,2,1024]{2,1,0:T(2,128)} %constant.8.clone.low_hbm), custom_call_target="tpu_custom_call" | custom-call | tf_op jit(solution)/shard_map/pallas_call | solution.py:359
  32.0 1.5 %copy.7 = f32[64,2,64]{2,1,0:T(2,128)} copy(f32[64,2,64]{2,1,0:T(2,128)} %shard_map.55) | data formatting | bytes 65536

commit v4 on v3

--- a/solution.py
+++ b/solution.py
@@ -121,6 +121,53 @@
     own[2:4] = rown[...]
 
     sends_next = jnp.logical_and(zh == 1, jnp.logical_and(d >= c.dop - c.tails, column < c.columns - 1))
+    peers = 2 * c.dop - 1 + 2 * (c.columns - 1)
+    pl.semaphore_wait(barrier, peers + jnp.where(sends_next, c.zs, 0))
+
+    def slice_copy(k):
+        to = at(2 * column + k // c.zl_count, 2 * (k % c.zl_count) + zh)
+        return pltpu.make_async_remote_copy(
+            src_ref=own, dst_ref=slots.at[c.tails + d], send_sem=s_send.at[k],
+            recv_sem=s_recv.at[c.tails + d], device_id=to, device_id_type=MESH)
+
+    def is_me(k, tm, dop_core):
+        return jnp.logical_and(
+            jnp.logical_and(tm == column, k == zh * c.zl_count + zl), dop_core == core)
+
+    next_block = t + 1
+    next_column, next_core = next_block // 2, lax.rem(next_block, 2)
+    sends_tail = jnp.logical_and(d >= c.dop - c.tails, next_block < c.tm)
+    tail_slot = jnp.maximum(d - (c.dop - c.tails), 0)
+
+    def tail_copy(k):
+        to = at(2 * next_column + k // c.zl_count, 2 * (k % c.zl_count) + next_core)
+        return pltpu.make_async_remote_copy(
+            src_ref=own, dst_ref=slots.at[tail_slot], send_sem=t_send.at[k],
+            recv_sem=s_recv.at[tail_slot], device_id=to, device_id_type=MESH)
+
+    for k in range(c.zs):
+        @pl.when(jnp.logical_not(is_me(k, column, zh)))
+        def _():
+            slice_copy(k).start()
+
+        @pl.when(jnp.logical_and(sends_tail, jnp.logical_not(is_me(k, next_column, next_core))))
+        def _():
+            tail_copy(k).start()
+
+    @pl.when(core == zh)
+    def _():
+        pltpu.make_async_copy(own, slots.at[c.tails + d], s_recv.at[c.tails + d]).start()
+
+    self_tail = jnp.logical_and(sends_tail, jnp.logical_and(next_column == column, next_core == core))
+
+    @pl.when(self_tail)
+    def _():
+        pltpu.make_async_copy(own, slots.at[tail_slot], s_recv.at[tail_slot]).start()
+
+    @pl.when(block == 0)
+    def _():
+        slots[: c.tails] = jnp.zeros((c.tails, 4, c.slice), jnp.bfloat16)
+
     for copy in tables:
         copy.wait()
     far_lanes = far.shape[-1]
@@ -140,53 +187,6 @@
         return carry
 
     lax.fori_loop(0, c.dop, phases, 0)
-
-    peers = 2 * c.dop - 1 + 2 * (c.columns - 1)
-    pl.semaphore_wait(barrier, peers + jnp.where(sends_next, c.zs, 0))
-
-    def slice_copy(k):
-        to = at(2 * column + k // c.zl_count, 2 * (k % c.zl_count) + zh)
-        return pltpu.make_async_remote_copy(
-            src_ref=own, dst_ref=slots.at[c.tails + d], send_sem=s_send.at[k],
-            recv_sem=s_recv.at[c.tails + d], device_id=to, device_id_type=MESH)
-
-    def is_me(k, tm, dop_core):
-        return jnp.logical_and(
-            jnp.logical_and(tm == column, k == zh * c.zl_count + zl), dop_core == core)
-
-    next_block = t + 1
-    next_column, next_core = next_block // 2, lax.rem(next_block, 2)
-    sends_tail = jnp.logical_and(d >= c.dop - c.tails, next_block < c.tm)
-    tail_slot = jnp.maximum(d - (c.dop - c.tails), 0)
-
-    def tail_copy(k):
-        to = at(2 * next_column + k // c.zl_count, 2 * (k % c.zl_count) + next_core)
-        return pltpu.make_async_remote_copy(
-            src_ref=own, dst_ref=slots.at[tail_slot], send_sem=t_send.at[k],
-            recv_sem=s_recv.at[tail_slot], device_id=to, device_id_type=MESH)
-
-    for k in range(c.zs):
-        @pl.when(jnp.logical_not(is_me(k, column, zh)))
-        def _():
-            slice_copy(k).start()
-
-        @pl.when(jnp.logical_and(sends_tail, jnp.logical_not(is_me(k, next_column, next_core))))
-        def _():
-            tail_copy(k).start()
-
-    @pl.when(core == zh)
-    def _():
-        pltpu.make_async_copy(own, slots.at[c.tails + d], s_recv.at[c.tails + d]).start()
-
-    self_tail = jnp.logical_and(sends_tail, jnp.logical_and(next_column == column, next_core == core))
-
-    @pl.when(self_tail)
-    def _():
-        pltpu.make_async_copy(own, slots.at[tail_slot], s_recv.at[tail_slot]).start()
-
-    @pl.when(block == 0)
-    def _():
-        slots[: c.tails] = jnp.zeros((c.tails, 4, c.slice), jnp.bfloat16)
 
     lane_no = lax.broadcasted_iota(jnp.int32, (8, LANES), 1)
     row_no = lax.broadcasted_iota(jnp.int32, (8, LANES), 0) + c.own_lags * zh
@@ -380,8 +380,8 @@
             dma((c.slot_count,)), dma((2 * c.columns,)), dma((c.tm,)),
         ],
         compiler_params=pltpu.CompilerParams(
-            collective_id=0, has_side_effects=True, vmem_limit_bytes=60 * 1024 * 1024),
-    )(surveillance.reshape(2, -1), reference_signal.reshape(2, -1), jnp.asarray(near), jnp.asarray(far), jnp.asarray(low))
+            collective_id=0, has_side_effects=True, vmem_limit_bytes=24 * 1024 * 1024),
+    )(*[pltpu.with_memory_space_constraint(v, pltpu.HBM) for v in (surveillance.reshape(2, -1), reference_signal.reshape(2, -1), jnp.asarray(near), jnp.asarray(far), jnp.asarray(low))])
 
 
 def solution(mesh, lags=2048, bins=512, side_y=4, side_x=4):

time: 33.7 us -> 31.7 us (0.941)
  Pallas kernels: 32 us -> 31 us
  local copies, waits for them, and re-layouts: 1.47 us -> 0.63 us
    pallas_call x1, Pallas kernels: 32 us -> 31 us  [run(): pl.pallas_call(functools.partial(kernel, c), out_shape=jax.ShapeDtypeStru...]
    unnamed x1, local copies, waits for them, and re-layouts: 1.47 us -> 0.63 us
where the time goes in v4:
time: 31.7 us; the launch traced here: 31.6 us
  Pallas kernels  31 us (98%)
  local copies, waits for them, and re-layouts  0.63 us (2%)
    pallas_call x1, Pallas kernels, run(): pl.pallas_call(functools.partial(kernel, c), out_shape=jax.ShapeDtypeStru...  31 us

profile of v4, /device:TPU:1, one launch (start us, length us, event | category | flops | bytes accessed | tf_op | source)
XLA Modules:
  0.0 31.6 jit_solution(4283995770320922247)
XLA Ops:
  0.0 31.0 %shard_map.55 = f32[64,2,64]{2,1,0:T(2,128)S(1)} custom-call(bf16[2,1024]{1,0:T(2,128)(2,1)} %bitcast.2, bf16[2,1024]{1,0:T(2,128)(2,1)} %bitcast.3, f32[2,128,1024]{2,1,0:T(8,128)} %constant.6.clone.near_hbm, f32[4,2,128,256]{3,2,1,0:T(8,128)} %constant.7.clone.far_hbm, f32[4,2,1024]{2,1,0:T(2,128)} %constant.8.clone.low_hbm), custom_call_target="tpu_custom_call" | custom-call | tf_op jit(solution)/shard_map/pallas_call | solution.py:359
  31.0 0.6 %copy.7 = f32[64,2,64]{2,1,0:T(2,128)} copy(f32[64,2,64]{2,1,0:T(2,128)S(1)} %shard_map.55) | data formatting | bytes 65536

commit v5 on v4

--- a/solution.py
+++ b/solution.py
@@ -11,7 +11,7 @@
 
 MESH = pl.DeviceIdType.MESH
 LANES = 128
-GROUP = 4
+GROUP = 5
 
 
 class Plan:
@@ -38,7 +38,7 @@
         def hops(o):
             return min(o[0], side_y - o[0]) + min(o[1], side_x - o[1])
 
-        self.offsets = sorted(offsets, key=lambda o: -hops(o))
+        self.offsets = sorted(offsets[1:], key=lambda o: -hops(o))
         self.zs = 2 * self.zl_count
 
 
@@ -96,19 +96,24 @@
     def greet(tm, dop):
         pl.semaphore_signal(barrier, inc=1, device_id=at(tm, dop), device_id_type=MESH)
 
-    for other_zh in range(2):
-        for other_d in range(c.dop):
-            @pl.when(jnp.logical_or(other_zh != zh, other_d != d))
-            def _():
-                greet(2 * column + other_zh, other_d)
+    z = zh * c.zl_count + zl
+    steps = sorted(range(c.zs), key=lambda o: -min(o, c.zs - o))
+
+    def along(step):
+        place = lax.rem(z + step, c.zs)
+        return place // c.zl_count, lax.rem(place, c.zl_count)
+
+    for step in steps:
+        there_zh, there_zl = along(step)
+        for other_core in [1 - core] if step == 0 else range(2):
+            greet(2 * column + there_zh, 2 * there_zl + other_core)
 
     def owner(offset):
         return lax.rem(y + offset[0], c.side_y) * c.side_x + lax.rem(xx + offset[1], c.side_x)
 
     for offset in c.offsets:
-        if offset != (0, 0):
-            for other_core in range(2):
-                greet(2 * owner(offset) + zh, 2 * zl + other_core)
+        for other_core in range(2):
+            greet(2 * owner(offset) + zh, 2 * zl + other_core)
 
     @pl.when(jnp.logical_and(core == 0, column > 0))
     def _():
@@ -117,56 +122,65 @@
 
     for copy in loads:
         copy.wait()
-    own[0:2] = sown[...]
-    own[2:4] = rown[...]
+    own[0] = sown[...]
+    own[1] = rown[...]
 
     sends_next = jnp.logical_and(zh == 1, jnp.logical_and(d >= c.dop - c.tails, column < c.columns - 1))
     peers = 2 * c.dop - 1 + 2 * (c.columns - 1)
     pl.semaphore_wait(barrier, peers + jnp.where(sends_next, c.zs, 0))
 
-    def slice_copy(k):
-        to = at(2 * column + k // c.zl_count, 2 * (k % c.zl_count) + zh)
+    def slice_copy(step):
+        there_zh, there_zl = along(step)
         return pltpu.make_async_remote_copy(
-            src_ref=own, dst_ref=slots.at[c.tails + d], send_sem=s_send.at[k],
-            recv_sem=s_recv.at[c.tails + d], device_id=to, device_id_type=MESH)
-
-    def is_me(k, tm, dop_core):
-        return jnp.logical_and(
-            jnp.logical_and(tm == column, k == zh * c.zl_count + zl), dop_core == core)
+            src_ref=own, dst_ref=slots.at[c.tails + d], send_sem=s_send.at[step],
+            recv_sem=s_recv.at[c.tails + d],
+            device_id=at(2 * column + there_zh, 2 * there_zl + zh), device_id_type=MESH)
 
     next_block = t + 1
     next_column, next_core = next_block // 2, lax.rem(next_block, 2)
     sends_tail = jnp.logical_and(d >= c.dop - c.tails, next_block < c.tm)
     tail_slot = jnp.maximum(d - (c.dop - c.tails), 0)
-
-    def tail_copy(k):
-        to = at(2 * next_column + k // c.zl_count, 2 * (k % c.zl_count) + next_core)
+    is_me = core == zh
+    tail_is_me = jnp.logical_and(next_column == column, next_core == core)
+
+    def tail_copy(step):
+        there_zh, there_zl = along(step)
         return pltpu.make_async_remote_copy(
-            src_ref=own, dst_ref=slots.at[tail_slot], send_sem=t_send.at[k],
-            recv_sem=s_recv.at[tail_slot], device_id=to, device_id_type=MESH)
-
-    for k in range(c.zs):
-        @pl.when(jnp.logical_not(is_me(k, column, zh)))
+            src_ref=own.at[1], dst_ref=slots.at[tail_slot, 1], send_sem=t_send.at[step],
+            recv_sem=s_recv.at[tail_slot],
+            device_id=at(2 * next_column + there_zh, 2 * there_zl + next_core),
+            device_id_type=MESH)
+
+    def each_send(act):
+        for step in steps:
+            def slice_part():
+                act(slice_copy(step))
+
+            slice_part() if step else pl.when(jnp.logical_not(is_me))(slice_part)
+
+        @pl.when(sends_tail)
         def _():
-            slice_copy(k).start()
-
-        @pl.when(jnp.logical_and(sends_tail, jnp.logical_not(is_me(k, next_column, next_core))))
-        def _():
-            tail_copy(k).start()
-
-    @pl.when(core == zh)
+            for step in steps:
+                def tail_part():
+                    act(tail_copy(step))
+
+                tail_part() if step else pl.when(jnp.logical_not(tail_is_me))(tail_part)
+
+    each_send(lambda copy: copy.start())
+
+    @pl.when(is_me)
     def _():
         pltpu.make_async_copy(own, slots.at[c.tails + d], s_recv.at[c.tails + d]).start()
 
-    self_tail = jnp.logical_and(sends_tail, jnp.logical_and(next_column == column, next_core == core))
+    self_tail = jnp.logical_and(sends_tail, tail_is_me)
 
     @pl.when(self_tail)
     def _():
-        pltpu.make_async_copy(own, slots.at[tail_slot], s_recv.at[tail_slot]).start()
+        pltpu.make_async_copy(own.at[1], slots.at[tail_slot, 1], s_recv.at[tail_slot]).start()
 
     @pl.when(block == 0)
     def _():
-        slots[: c.tails] = jnp.zeros((c.tails, 4, c.slice), jnp.bfloat16)
+        slots[: c.tails, 1] = jnp.zeros((c.tails, 2, c.slice), jnp.bfloat16)
 
     for copy in tables:
         copy.wait()
@@ -197,13 +211,16 @@
     def wait_slot(slot):
         pltpu.make_async_copy(own, slots.at[slot], s_recv.at[slot]).wait()
 
+    def wait_tail(slot):
+        pltpu.make_async_copy(own.at[1], slots.at[slot, 1], s_recv.at[slot]).wait()
+
     def shifts(slot):
-        both = slots[slot].astype(jnp.float32)
-        for part in (2, 3):
+        both = slots[slot, 1].astype(jnp.float32)
+        for part in range(2):
             for high in range(0, c.own_lags, 16):
                 groups = (high // 8, high // 8 + 1)
                 keep = jnp.concatenate([own_part[g] for g in groups], 0)
-                rows = slice((part - 2) * c.own_lags + high, (part - 2) * c.own_lags + high + 16)
+                rows = slice(part * c.own_lags + high, part * c.own_lags + high + 16)
                 last = None
                 for tile in range(c.slice // LANES + 1):
                     place = pl.ds(pl.multiple_of(slot * c.slice + tile * LANES, LANES), LANES)
@@ -220,7 +237,7 @@
                     last = turned
 
     def mixing(k):
-        both = slots[c.tails + k].astype(jnp.float32)
+        both = slots[c.tails + k, 0].astype(jnp.float32)
         lre, lim = low[0:1], low[1:2]
         sre = both[0:1] * lre - both[1:2] * lim
         sim = both[0:1] * lim + both[1:2] * lre
@@ -252,7 +269,7 @@
     @pl.when(block > 0)
     def _():
         for k in range(c.tails):
-            wait_slot(k)
+            wait_tail(k)
 
     def tail_shifts(slot, carry):
         shifts(slot)
@@ -261,8 +278,8 @@
     lax.fori_loop(0, c.tails, tail_shifts, 0)
 
     sign = jnp.where(lax.broadcasted_iota(jnp.int32, (1, LANES), 1) < c.own_bins, 1.0, -1.0)
-    members = min(GROUP, c.columns)
-    groups = c.columns // members
+    members = min(GROUP, c.columns - 1)
+    groups = (c.columns - 1) // members
 
     def offset_of(group, member):
         def digit(axis, side):
@@ -282,72 +299,71 @@
             device_id=at(2 * owner(offset_of(group, member)) + zh, 2 * zl + other_core),
             device_id_type=MESH)
 
-    def stays(group, member, other_core):
-        last = jnp.logical_and(group == groups - 1, core == other_core)
-        return last if member == members - 1 else False
+    def window(to):
+        return toep[:, pl.ds(pl.multiple_of(c.tails * c.slice - LANES * to, LANES), c.block)]
+
+    def times(rows, columns):
+        return lax.dot_general(
+            rows, columns, (((1,), (1,)), ((), ())), preferred_element_type=jnp.float32)
+
+    def piece_of(product, top, other_core):
+        cols = slice(other_core * LANES, (other_core + 1) * LANES)
+        a = product[top : top + c.own_lags, cols]
+        b = product[top + c.own_lags : top + 2 * c.own_lags, cols]
+        return a + pltpu.roll(b, c.own_bins, 1) * sign
 
     def products(group, carry):
-        windows = []
+        windows = [window(owner(offset_of(group, member))) for member in range(members)]
+        product = times(jnp.concatenate(windows, 0), x[...])
         for member in range(members):
-            to = owner(offset_of(group, member))
-            windows.append(toep[:, pl.ds(pl.multiple_of(c.tails * c.slice - LANES * to, LANES), c.block)])
-        product = lax.dot_general(
-            jnp.concatenate(windows, 0), x[...], (((1,), (1,)), ((), ())),
-            preferred_element_type=jnp.float32)
+            for other_core in range(2):
+                piece = piece_of(product, member * 2 * c.own_lags, other_core)
+                outbox[2 * (group * members + member) + other_core] = piece.astype(jnp.bfloat16)
+                piece_copy(group, member, other_core).start()
+        return carry
+
+    lax.fori_loop(0, groups, products, 0)
+
+    product = jnp.transpose(times(x[...], window(column)))
+    pieces = [piece_of(product, 0, other_core) for other_core in range(2)]
+    kept[...] = jnp.where(core == 0, pieces[0], pieces[1])
+    partner_slot = 2 * (c.columns - 1)
+    outbox[partner_slot] = jnp.where(core == 0, pieces[1], pieces[0]).astype(jnp.bfloat16)
+    partner_copy = pltpu.make_async_remote_copy(
+        src_ref=outbox.at[partner_slot], dst_ref=inbox.at[block], send_sem=p_send.at[partner_slot],
+        recv_sem=p_recv.at[block], device_id=at(t, 2 * zl + 1 - core), device_id_type=MESH)
+    partner_copy.start()
+
+    def take(n):
+        pltpu.make_async_copy(outbox.at[0], inbox.at[n], p_recv.at[n]).wait()
+        kept[...] += inbox[n].astype(jnp.float32)
+
+    def collect(group, carry):
         for member in range(members):
-            top = member * 2 * c.own_lags
+            offset = offset_of(group, member)
+            source = lax.rem(y + c.side_y - offset[0], c.side_y) * c.side_x + lax.rem(
+                xx + c.side_x - offset[1], c.side_x)
             for other_core in range(2):
-                cols = slice(other_core * LANES, (other_core + 1) * LANES)
-                a = product[top : top + c.own_lags, cols]
-                b = product[top + c.own_lags : top + 2 * c.own_lags, cols]
-                piece = a + pltpu.roll(b, c.own_bins, 1) * sign
-                outbox[2 * (group * members + member) + other_core] = piece.astype(jnp.bfloat16)
-                if member < members - 1:
-                    piece_copy(group, member, other_core).start()
-                else:
-                    here = stays(group, member, other_core)
-
-                    @pl.when(here)
-                    def _():
-                        kept[...] = piece
-
-                    @pl.when(jnp.logical_not(here))
-                    def _():
-                        piece_copy(group, member, other_core).start()
-        return carry
-
-    lax.fori_loop(0, groups, products, 0)
-
+                take(2 * source + other_core)
+        return carry
+
+    lax.fori_loop(0, groups, collect, 0)
+    take(2 * column + 1 - core)
     total = kept[...]
-    for offset in c.offsets:
-        source = lax.rem(y + c.side_y - offset[0], c.side_y) * c.side_x + lax.rem(
-            xx + c.side_x - offset[1], c.side_x)
-        for n in [2 * source + 1 - core] if offset == (0, 0) else [2 * source, 2 * source + 1]:
-            pltpu.make_async_copy(outbox.at[0], inbox.at[n], p_recv.at[n]).wait()
-            total = total + inbox[n].astype(jnp.float32)
-
     total = total * (1.0 / math.sqrt(c.window))
     out_ref[:, 0, :] = total[:, : c.own_bins]
     out_ref[:, 1, :] = total[:, c.own_bins :]
 
-    for k in range(c.zs):
-        @pl.when(jnp.logical_not(is_me(k, column, zh)))
-        def _():
-            slice_copy(k).wait_send()
-
-        @pl.when(jnp.logical_and(sends_tail, jnp.logical_not(is_me(k, next_column, next_core))))
-        def _():
-            tail_copy(k).wait_send()
+    each_send(lambda copy: copy.wait_send())
 
     def left(group, carry):
         for member in range(members):
             for other_core in range(2):
-                @pl.when(jnp.logical_not(stays(group, member, other_core)))
-                def _():
-                    piece_copy(group, member, other_core).wait_send()
+                piece_copy(group, member, other_core).wait_send()
         return carry
 
     lax.fori_loop(0, groups, left, 0)
+    partner_copy.wait_send()
 
 
 def run(plan, surveillance, reference_signal):
@@ -364,8 +380,8 @@
         scratch_shapes=[
             pltpu.VMEM((2, c.slice), bf16),
             pltpu.VMEM((2, c.slice), bf16),
-            pltpu.VMEM((4, c.slice), bf16),
-            pltpu.VMEM((c.slot_count, 4, c.slice), bf16),
+            pltpu.VMEM((2, 2, c.slice), bf16),
+            pltpu.VMEM((c.slot_count, 2, 2, c.slice), bf16),
             pltpu.VMEM(near.shape, f32),
             pltpu.VMEM(far.shape[1:], f32),
             pltpu.VMEM(low.shape[1:], f32),

time: 31.7 us -> 30.8 us (0.972)
  Pallas kernels: 31 us -> 30 us
    pallas_call x1, Pallas kernels: 31 us -> 30 us  [run(): pl.pallas_call(functools.partial(kernel, c), out_shape=jax.ShapeDtypeStru...]
where the time goes in v5:
time: 30.8 us; the launch traced here: 30.7 us
  Pallas kernels  30 us (97%)
  local copies, waits for them, and re-layouts  0.63 us (2%)
    pallas_call x1, Pallas kernels, run(): pl.pallas_call(functools.partial(kernel, c), out_shape=jax.ShapeDtypeStru...  30 us
    unnamed x1, local copies, waits for them, and re-layouts  0.63 us

profile of v5, /device:TPU:1, one launch (start us, length us, event | category | flops | bytes accessed | tf_op | source)
XLA Modules:
  0.0 30.7 jit_solution(13410268624556939579)
XLA Ops:
  0.0 30.0 %shard_map.55 = f32[64,2,64]{2,1,0:T(2,128)S(1)} custom-call(bf16[2,1024]{1,0:T(2,128)(2,1)} %bitcast.2, bf16[2,1024]{1,0:T(2,128)(2,1)} %bitcast.3, f32[2,128,1024]{2,1,0:T(8,128)} %constant.6.clone.near_hbm, f32[4,2,128,256]{3,2,1,0:T(8,128)} %constant.7.clone.far_hbm, f32[4,2,1024]{2,1,0:T(2,128)} %constant.8.clone.low_hbm), custom_call_target="tpu_custom_call" | custom-call | tf_op jit(solution)/shard_map/pallas_call | solution.py:375
  30.0 0.6 %copy.7 = f32[64,2,64]{2,1,0:T(2,128)} copy(f32[64,2,64]{2,1,0:T(2,128)S(1)} %shard_map.55) | data formatting | bytes 65536
